TPU v7x, 512 devices: a 8x2x16 block of a 8x8x16 slice. The times are simulated.
512 devices in a mesh: groups: 2 (over y), ffn: 16 (over x, core), width: 16 (over z).
Axes of the slice: x: 8, y: 2, z: 16, core: 2. Of those that a mesh axis runs over, the one named last changes fastest.
The devices are a block of a 8x8x16 slice.
Arguments:
- hidden: bfloat16 [2048, 8192], P(('groups', 'ffn'), 'width'), parts along dimension 0, may hold values from -8.4 to 8.4
- upstream: bfloat16 [2048, 8192], P(('groups', 'ffn'), 'width'), parts along dimension 0, may hold values from -6 to 6
- query_frozen_weight: bfloat16 [8192, 8192], P('width', 'ffn'), may hold values from -0.0625 to 0.0625
- key_value_frozen_weight: bfloat16 [2, 8192, 1024], P(None, 'width', 'ffn'), may hold values from -0.0625 to 0.0625
- output_frozen_weight: bfloat16 [8192, 8192], P('ffn', 'width'), may hold values from -0.0625 to 0.0625
- adapter_down: bfloat16 [6, 16, 8192], P('groups', None, 'width'), parts along dimension 0, may hold values from -0.0625 to 0.0625
- query_up_map: bfloat16 [32, 8192], P('groups', 'ffn'), parts along dimension 0, may hold values from -0.0625 to 0.0625
- key_value_up_maps: bfloat16 [4, 16, 1024], P('groups', None, 'ffn'), parts along dimension 0, may hold values from -0.0625 to 0.0625
- output_down_map: bfloat16 [32, 8192], P('groups', 'ffn'), parts along dimension 0, may hold values from -0.0625 to 0.0625
- output_up: bfloat16 [32, 8192], P('groups', 'width'), parts along dimension 0, may hold values from -0.0625 to 0.0625
Outputs:
- hidden_gradient: bfloat16 [2048, 8192], P(('groups', 'ffn'), 'width'), parts along dimension 0
- down_map_gradient: float32 [6, 16, 8192], P('groups', None, 'width'), parts along dimension 0
- query_up_map_gradient: float32 [32, 8192], P('groups', 'ffn'), parts along dimension 0
- key_value_up_maps_gradient: float32 [4, 16, 1024], P('groups', None, 'ffn'), parts along dimension 0
- output_down_map_gradient: float32 [32, 8192], P('groups', 'ffn'), parts along dimension 0
- output_up_map_gradient: float32 [32, 8192], P('groups', 'width'), parts along dimension 0
There are 2 independent parts, one for each index of `groups`. A program takes and returns all parts, laid end to end along the dimension named above; an argument that names none is the same for every part. Nothing has to cross between parts.
All inputs are finite; a program needn't handle non-finite values.
Results may differ from a plain program's by a relative error of at most 0.04.
Values may be sent and summed in bfloat16 or wider, within the bound.
No kernel may reach another device: no remote copies, remote signals or barrier semaphores. Data moves between devices by JAX's collectives and lax.ppermute only.
A program may use at most 64 MiB of HBM per device.

v0:
```python
import math

import jax
import jax.numpy as jnp
from jax import lax
from jax.sharding import PartitionSpec as P

HEAD_DIM = 128
ADAPTER_RANK = 16


adapter_scale = 2.0
rope_base = 500000.0


def in_one_piece(arrays, axis, dim, along):
    both = jnp.concatenate(arrays, axis=along)
    out, at, gathered = (lax.all_gather(both, axis, axis=dim, tiled=True), 0, [])
    for a in arrays:
        gathered.append(lax.slice_in_dim(out, at, at + a.shape[along], axis=along))
        at += a.shape[along]
    return tuple(gathered)


def gathered_total(array, axis):
    return lax.all_gather(array, axis).sum(0)


def split_up(array, dim, size):
    shape = array.shape
    pieces = array.reshape(*shape[:dim], size, shape[dim] // size, *shape[dim + 1 :])
    return jnp.moveaxis(pieces, dim, 0)


def sum_at_owner(array, axis, dim):
    pieces = split_up(array, dim, lax.axis_size(axis))
    arrived = lax.all_to_all(pieces, axis, split_axis=0, concat_axis=0, tiled=True)
    return arrived.astype(jnp.float32).sum(axis=0)


def sent_together(arrays, axis, dim, along):
    widths = [a.shape[along] for a in arrays]
    both = jnp.concatenate(arrays, axis=along)
    out = sum_at_owner(both, axis, dim)
    return tuple(jnp.split(out, [sum(widths[:k]) for k in range(1, len(widths))], axis=along))


def from_partner(array, axis, bit):
    return lax.ppermute(array, axis, [(i, i ^ 1 << bit) for i in range(lax.axis_size(axis))])


def sent_and_summed(array, axis, dim):
    pieces = split_up(array, dim, lax.axis_size(axis))
    arrived = lax.all_to_all(pieces, axis, split_axis=0, concat_axis=0, tiled=True)
    return arrived.sum(axis=0)


def sent_together_2(arrays, axis, dim, along):
    both = jnp.concatenate(arrays, axis=along)
    out, at, gathered = (sent_and_summed(both, axis, dim), 0, [])
    for a in arrays:
        gathered.append(lax.slice_in_dim(out, at, at + a.shape[along], axis=along))
        at += a.shape[along]
    return tuple(gathered)


def in_order(pieces, dim):
    shape = list(pieces.shape[1:])
    shape[dim] *= pieces.shape[0]
    return jnp.moveaxis(pieces, 0, dim).reshape(shape)


def from_everyone(array, axis):
    size = lax.axis_size(axis)
    return lax.all_to_all(
        jnp.broadcast_to(array[None], (size, *array.shape)), axis, 0, 0, tiled=True
    )


def gathered_copies(array, axis, dim):
    return in_order(from_everyone(array, axis), dim)


def taken_together(array, axis):
    return from_everyone(array, axis).sum(axis=0)


def rotate(values, positions, first_dim, direction):
    columns = values.shape[1]
    head_dims = (first_dim + jnp.arange(columns, dtype=jnp.int32)) % HEAD_DIM
    pair_dims = head_dims - head_dims % 2
    frequency = jnp.exp(pair_dims.astype(jnp.float32) * (-math.log(rope_base) / HEAD_DIM))
    angles = positions.astype(jnp.float32)[:, None] * frequency[None, :]
    is_even = head_dims % 2 == 0
    following = jnp.roll(values, -1, axis=1)
    preceding = jnp.roll(values, 1, axis=1)
    partner = jnp.where(is_even[None, :], -following, preceding)
    return values * jnp.cos(angles) + direction * partner * jnp.sin(angles)


def contract_last(left_side, right_side):
    return lax.dot_general(
        left_side, right_side, (((1,), (1,)), ((), ())), preferred_element_type=jnp.float32
    )


def contract_leading(left_side, right_side):
    return lax.dot_general(
        left_side, right_side, (((0,), (0,)), ((), ())), preferred_element_type=jnp.float32
    )


def shards(
    hidden,
    upstream,
    query_frozen_weight,
    key_value_frozen_weight,
    output_frozen_weight,
    adapter_down,
    query_up_map,
    key_value_up_maps,
    output_down_map,
    output_up,
):
    ffn_count = lax.axis_size("ffn")
    width_count = lax.axis_size("width")
    ffn_index = lax.axis_index("ffn")
    width_index = lax.axis_index("width")
    hidden_rows_full, upstream_gradient_full = in_one_piece((hidden, upstream), "ffn", 0, 1)
    token_count = hidden_rows_full.shape[0]
    query_rows = token_count // width_count
    query_cols = query_frozen_weight.shape[1]
    key_cols = key_value_frozen_weight.shape[2]
    row_start = width_index * query_rows
    positions = jnp.arange(token_count, dtype=jnp.int32)
    row_positions = row_start + jnp.arange(query_rows, dtype=jnp.int32)
    query_offset = ffn_index * query_cols
    key_offset = ffn_index * key_cols
    score_scale = 1.0 / math.sqrt(HEAD_DIM)
    down_flattened = adapter_down.reshape(3 * ADAPTER_RANK, adapter_down.shape[2])
    parity = ffn_index % 2
    rank_terms = contract_last(hidden_rows_full, down_flattened)
    upstream_terms = contract_last(upstream_gradient_full, output_up)
    rank_sum, upstream_sum = (
        gathered_total(rank_terms, "width"),
        gathered_total(upstream_terms, "width"),
    )
    reduced_hidden = rank_sum.astype(jnp.bfloat16)
    output_reduced = upstream_sum.astype(jnp.bfloat16)
    low_rows = lax.dynamic_slice_in_dim(reduced_hidden, row_start, query_rows, 0)
    output_token_rows = lax.dynamic_slice_in_dim(output_reduced, row_start, query_rows, 0)
    query_part = jnp.dot(hidden_rows_full, query_frozen_weight, preferred_element_type=jnp.float32)
    query_gradient_summed = sum_at_owner(query_part.astype(jnp.bfloat16), "width", 0)
    query_projected = query_gradient_summed + adapter_scale * jnp.dot(
        low_rows[:, :ADAPTER_RANK], query_up_map, preferred_element_type=jnp.float32
    )
    query_states = rotate(query_projected, row_positions, query_offset, 1.0).astype(jnp.bfloat16)
    key_part = jnp.dot(
        hidden_rows_full, key_value_frozen_weight[0], preferred_element_type=jnp.float32
    )
    value_part = jnp.dot(
        hidden_rows_full, key_value_frozen_weight[1], preferred_element_type=jnp.float32
    )
    key_gradient_summed, value_gradient_summed = sent_together(
        (key_part.astype(jnp.bfloat16), value_part.astype(jnp.bfloat16)), "width", 0, 1
    )
    key_projected = key_gradient_summed + adapter_scale * jnp.dot(
        low_rows[:, ADAPTER_RANK : 2 * ADAPTER_RANK],
        key_value_up_maps[0],
        preferred_element_type=jnp.float32,
    )
    value_projected = value_gradient_summed + adapter_scale * jnp.dot(
        low_rows[:, 2 * ADAPTER_RANK :], key_value_up_maps[1], preferred_element_type=jnp.float32
    )
    key_block = rotate(key_projected, row_positions, key_offset, 1.0).astype(jnp.bfloat16)
    value_block = value_projected.astype(jnp.bfloat16)
    key_states, value_state_rows = in_one_piece((key_block, value_block), "width", 0, 1)
    other_key, other_value = from_partner((key_states, value_state_rows), "ffn", 0)
    key_states = jnp.where(
        parity == 0,
        jnp.concatenate([key_states, other_key], 1),
        jnp.concatenate([other_key, key_states], 1),
    )
    value_state_rows = jnp.where(
        parity == 0,
        jnp.concatenate([value_state_rows, other_value], 1),
        jnp.concatenate([other_value, value_state_rows], 1),
    )
    local_heads = query_cols // HEAD_DIM
    local_groups = key_states.shape[1] // HEAD_DIM
    group_size = local_heads // local_groups
    query_four = query_states.reshape(query_rows, local_groups, group_size, HEAD_DIM)
    key_three = key_states.reshape(token_count, local_groups, HEAD_DIM)
    value_three = value_state_rows.reshape(token_count, local_groups, HEAD_DIM)
    causal = row_positions[:, None] >= positions[None, :]
    scores = (
        jnp.einsum("qkgd,skd->kgqs", query_four, key_three, preferred_element_type=jnp.float32)
        * score_scale
    )
    scores = jnp.where(causal[None, None, :, :], scores, -jnp.inf)
    shifted = jnp.exp(scores - jnp.max(scores, axis=-1, keepdims=True))
    probs = shifted / jnp.sum(shifted, axis=-1, keepdims=True)
    prob_weights = probs.astype(jnp.bfloat16)
    attention_four = jnp.einsum(
        "kgqs,skd->qkgd", prob_weights, value_three, preferred_element_type=jnp.float32
    ).astype(jnp.bfloat16)
    attention_output = attention_four.reshape(query_rows, query_cols)
    out_part = contract_last(upstream_gradient_full, output_frozen_weight)
    output_gradient_summed = sum_at_owner(out_part.astype(jnp.bfloat16), "width", 0)
    attention_output_gradient = (
        output_gradient_summed
        + adapter_scale
        * jnp.dot(output_token_rows, output_down_map, preferred_element_type=jnp.float32)
    ).astype(jnp.bfloat16)
    grad_four = attention_output_gradient.reshape(query_rows, local_groups, group_size, HEAD_DIM)
    prob_grad = jnp.einsum(
        "qkgd,skd->kgqs", grad_four, value_three, preferred_element_type=jnp.float32
    )
    delta = jnp.einsum(
        "qkgd,qkgd->kgq", grad_four, attention_four, preferred_element_type=jnp.float32
    )
    score_grad = (probs * (prob_grad - delta[:, :, :, None]) * score_scale).astype(jnp.bfloat16)
    query_rot_grad = jnp.einsum(
        "kgqs,skd->qkgd", score_grad, key_three, preferred_element_type=jnp.float32
    ).reshape(query_rows, query_cols)
    key_part_grad = jnp.einsum(
        "kgqs,qkgd->skd", score_grad, query_four, preferred_element_type=jnp.float32
    ).reshape(token_count, local_groups * HEAD_DIM)
    value_part_grad = jnp.einsum(
        "kgqs,qkgd->skd", prob_weights, grad_four, preferred_element_type=jnp.float32
    ).reshape(token_count, local_groups * HEAD_DIM)
    query_block_grad = rotate(query_rot_grad, row_positions, query_offset, -1.0).astype(
        jnp.bfloat16
    )

    def own_half(values):
        return lax.dynamic_slice_in_dim(values, parity * key_cols, key_cols, 1)

    def other_half(values):
        return lax.dynamic_slice_in_dim(values, (1 - parity) * key_cols, key_cols, 1)

    key_total, value_total = (key_part_grad, value_part_grad)
    sent_key, sent_value = from_partner((other_half(key_total), other_half(value_total)), "ffn", 0)
    key_total = own_half(key_total) + sent_key
    value_total = own_half(value_total) + sent_value
    key_rows_sum, value_rows_sum = sent_together_2((key_total, value_total), "width", 0, 1)
    key_finished = rotate(key_rows_sum, row_positions, key_offset, -1.0).astype(jnp.bfloat16)
    value_finished = value_rows_sum.astype(jnp.bfloat16)
    key_rows_gradient, value_rows_gradient = in_one_piece(
        (key_finished, value_finished), "width", 0, 1
    )
    query_rows_gradient = gathered_copies(query_block_grad, "width", 0)
    input_part = (
        contract_last(query_rows_gradient, query_frozen_weight)
        + contract_last(key_rows_gradient, key_value_frozen_weight[0])
        + contract_last(value_rows_gradient, key_value_frozen_weight[1])
    )
    rank_grad_terms = jnp.concatenate(
        [
            contract_last(query_rows_gradient, query_up_map),
            contract_last(key_rows_gradient, key_value_up_maps[0]),
            contract_last(value_rows_gradient, key_value_up_maps[1]),
        ],
        axis=1,
    )
    rank_gradient = gathered_total(rank_grad_terms, "ffn").astype(jnp.bfloat16)
    input_sum = sum_at_owner(input_part.astype(jnp.bfloat16), "ffn", 0)
    own_rows = token_count // ffn_count
    rank_gradient_token_rows = lax.dynamic_slice_in_dim(
        rank_gradient, ffn_index * own_rows, own_rows, 0
    )
    hidden_gradient = (
        input_sum
        + adapter_scale
        * jnp.dot(rank_gradient_token_rows, down_flattened, preferred_element_type=jnp.float32)
    ).astype(jnp.bfloat16)
    down_map_gradient = (adapter_scale * contract_leading(rank_gradient, hidden_rows_full)).reshape(
        adapter_down.shape
    )
    query_up_map_gradient = adapter_scale * contract_leading(
        reduced_hidden[:, :ADAPTER_RANK], query_rows_gradient
    )
    key_value_up_maps_gradient = adapter_scale * jnp.stack(
        [
            contract_leading(reduced_hidden[:, ADAPTER_RANK : 2 * ADAPTER_RANK], key_rows_gradient),
            contract_leading(reduced_hidden[:, 2 * ADAPTER_RANK :], value_rows_gradient),
        ]
    )
    outer_terms = contract_last(attention_output, output_down_map)
    outer_rows = taken_together(outer_terms, "ffn").astype(jnp.bfloat16)
    outer_product_rank = gathered_copies(outer_rows, "width", 0)
    output_down_map_gradient = adapter_scale * taken_together(
        contract_leading(output_token_rows, attention_output), "width"
    )
    output_up_map_gradient = adapter_scale * contract_leading(
        outer_product_rank, upstream_gradient_full
    )
    return (
        hidden_gradient,
        down_map_gradient,
        query_up_map_gradient,
        key_value_up_maps_gradient,
        output_down_map_gradient,
        output_up_map_gradient,
    )


def solution(mesh):
    placed = (
        P(("groups", "ffn"), "width"),
        P(("groups", "ffn"), "width"),
        P("width", "ffn"),
        P(None, "width", "ffn"),
        P("ffn", "width"),
        P("groups", None, "width"),
        P("groups", "ffn"),
        P("groups", None, "ffn"),
        P("groups", "ffn"),
        P("groups", "width"),
    )
    return jax.shard_map(
        shards,
        mesh=mesh,
        in_specs=placed,
        out_specs=(
            P(("groups", "ffn"), "width"),
            P("groups", None, "width"),
            P("groups", "ffn"),
            P("groups", None, "ffn"),
            P("groups", "ffn"),
            P("groups", "width"),
        ),
        check_vma=False,
    )
```

profile of v0, /device:TPU:65, one launch (start us, length us, event | category | flops | bytes accessed | tf_op | source)
XLA Modules:
  0.0 600.8 jit_solution(13749118733938458724)
XLA Ops:
  8.9 81.6 %all-gather.8.cloned.1.call-done = bf16[1024,1024]{1,0:T(8,128)(2,1)} async-done(((bf16[64,1024]{1,0:T(8,128)(2,1)}), bf16[1024,1024]{1,0:T(8,128)(2,1)}) %all-gather.8.cloned.1.call-update) | async-done | bytes 2097168 | tf_op jit(solution)/shard_map/all_gather | solution.py:18
  94.8 13.0 %all-to-all-start = ((bf16[16,64,128]{2,1,0:T(8,128)(2,1)}), bf16[16,64,128]{2,1,0:T(8,128)(2,1)S(1)}, u32[]{:S(2)}, u32[]{:S(2)}) async-start(bf16[16,64,128]{2,1,0:T(8,128)(2,1)} %bitcast.4), calls=%async_computation | async-start | bytes 524288 | tf_op jit(solution)/shard_map/all_to_all | solution.py:37
  109.6 12.1 %all-to-all-done = bf16[16,64,128]{2,1,0:T(8,128)(2,1)S(1)} async-done(((bf16[16,64,128]{2,1,0:T(8,128)(2,1)}), bf16[16,64,128]{2,1,0:T(8,128)(2,1)S(1)}, u32[]{:S(2)}, u32[]{:S(2)}) %all-to-all-start) | async-done | bytes 262176 | tf_op jit(solution)/shard_map/all_to_all | solution.py:37
  121.7 10.4 %all-to-all-start.2 = ((bf16[16,64,512]{2,1,0:T(8,128)(2,1)}), bf16[16,64,512]{2,1,0:T(8,128)(2,1)S(1)}, u32[]{:S(2)}, u32[]{:S(2)}) async-start(bf16[16,64,512]{2,1,0:T(8,128)(2,1)} %bitcast.13), calls=%async_computation.2 | async-start | bytes 2097152 | tf_op jit(solution)/shard_map/all_to_all | solution.py:37
  140.0 40.6 %all-to-all-done.2 = bf16[16,64,512]{2,1,0:T(8,128)(2,1)S(1)} async-done(((bf16[16,64,512]{2,1,0:T(8,128)(2,1)}), bf16[16,64,512]{2,1,0:T(8,128)(2,1)S(1)}, u32[]{:S(2)}, u32[]{:S(2)}) %all-to-all-start.2) | async-done | bytes 1048608 | tf_op jit(solution)/shard_map/all_to_all | solution.py:37
  180.6 13.9 %all-to-all-start.1 = ((bf16[16,64,512]{2,1,0:T(8,128)(2,1)}), bf16[16,64,512]{2,1,0:T(8,128)(2,1)S(1)}, u32[]{:S(2)}, u32[]{:S(2)}) async-start(bf16[16,64,512]{2,1,0:T(8,128)(2,1)} %bitcast.204), calls=%async_computation.1 | async-start | bytes 2097152 | tf_op jit(solution)/shard_map/all_to_all | solution.py:37
  195.5 27.1 %all-gather.12.cloned.1.call-done = f32[16384,16]{0,1:T(8,128)} async-done(((f32[1024,16]{0,1:T(8,128)}), f32[16384,16]{0,1:T(8,128)}) %all-gather.12.cloned.1.call-update) | async-done | bytes 1048592 | tf_op jit(solution)/shard_map/all_gather | solution.py:26
  225.5 18.2 %all-to-all-done.1 = bf16[16,64,512]{2,1,0:T(8,128)(2,1)S(1)} async-done(((bf16[16,64,512]{2,1,0:T(8,128)(2,1)}), bf16[16,64,512]{2,1,0:T(8,128)(2,1)S(1)}, u32[]{:S(2)}, u32[]{:S(2)}) %all-to-all-start.1) | async-done | bytes 1048608 | tf_op jit(solution)/shard_map/all_to_all | solution.py:37
  243.9 58.8 %all-gather.10.cloned.1.call-done = f32[16384,48]{0,1:T(8,128)} async-done(((f32[1024,48]{0,1:T(8,128)}), f32[16384,48]{0,1:T(8,128)}) %all-gather.10.cloned.1.call-update) | async-done | bytes 3145744 | tf_op jit(solution)/shard_map/all_gather | solution.py:26
  302.7 3.7 copy.132
  308.5 22.0 %all_gather.30 = bf16[1024,128]{1,0:T(8,128)(2,1)S(1)} all-gather(bf16[64,128]{1,0:T(8,128)(2,1)S(1)} %pad_maximum_fusion.4), channel_id=1, replica_groups=mesh['groups'=2,'ffn'=16,'width'=16] {'width'}, dimensions={0}, use_global_device_ids=true | all-gather | bytes 278528 | tf_op jit(solution)/shard_map/all_gather | solution.py:18
  330.7 19.5 %collective-permute-start.1 = (bf16[1024,64]{1,0:T(8,128)(2,1)S(1)}, bf16[1024,64]{1,0:T(8,128)(2,1)S(1)}, u32[]{:S(2)}, u32[]{:S(2)}) collective-permute-start(bf16[1024,64]{1,0:T(8,128)(2,1)S(1)} %get-tuple-element.6), channel_id=1, source_target_pairs={{0,16},{16,0},{32,48},{48,32},{64,80},{80,64},{96,112},{112,96},{1... | collective-permute-start | bytes 393224 | tf_op jit(solution)/shard_map/ppermute | solution.py:49
  365.1 6.8 %all-to-all-start.4 = ((f32[16,64,128]{2,1,0:T(8,128)}), f32[16,64,128]{2,1,0:T(8,128)S(1)}, u32[]{:S(2)}, u32[]{:S(2)}) async-start(f32[16,64,128]{2,1,0:T(8,128)} %bitcast.41), calls=%async_computation.4 | async-start | bytes 1048576 | tf_op jit(solution)/shard_map/all_to_all | solution.py:54
  373.3 21.1 %all-to-all-done.4 = f32[16,64,128]{2,1,0:T(8,128)S(1)} async-done(((f32[16,64,128]{2,1,0:T(8,128)}), f32[16,64,128]{2,1,0:T(8,128)S(1)}, u32[]{:S(2)}, u32[]{:S(2)}) %all-to-all-start.4) | async-done | bytes 524320 | tf_op jit(solution)/shard_map/all_to_all | solution.py:54
  395.5 13.0 %all-to-all-start.3 = ((bf16[16,64,512]{2,1,0:T(8,128)(2,1)}), bf16[16,64,512]{2,1,0:T(8,128)(2,1)S(1)}, u32[]{:S(2)}, u32[]{:S(2)}) async-start(bf16[16,64,512]{2,1,0:T(8,128)(2,1)} %broadcast_in_dim.46), calls=%async_computation.3 | async-start | bytes 2097152 | tf_op jit(solution)/shard_map/all_to_all | solution.py:75
  409.2 65.3 %all_gather.33 = bf16[1024,128]{1,0:T(8,128)(2,1)S(1)} all-gather(bf16[64,128]{1,0:T(8,128)(2,1)S(1)} %pad_maximum_fusion.5), channel_id=1, replica_groups=mesh['groups'=2,'ffn'=16,'width'=16] {'width'}, dimensions={0}, use_global_device_ids=true | all-gather | bytes 278528 | tf_op jit(solution)/shard_map/all_gather | solution.py:18
  476.4 21.4 %all_to_all.45 = f32[16,1,1024]{2,1,0:T(1,128)S(1)} all-to-all(f32[16,1,1024]{2,1,0:T(1,128)S(1)} %reshape.371), channel_id=1, replica_groups=mesh['groups'=2,'ffn'=16,'width'=16] {'ffn'}, dimensions={0} | all-to-all | bytes 131072 | tf_op jit(solution)/shard_map/all_to_all | solution.py:75
  500.0 10.3 %all-to-all-start.8 = ((bf16[16,2,512]{2,1,0:T(2,128)(2,1)}), bf16[16,2,512]{2,1,0:T(2,128)(2,1)S(1)}, u32[]{:S(2)}, u32[]{:S(2)}) async-start(bf16[16,2,512]{2,1,0:T(2,128)(2,1)} %reshape.373), calls=%async_computation.8 | async-start | bytes 65536 | tf_op jit(solution)/shard_map/all_to_all | solution.py:75
  511.2 10.5 %all-to-all-done.8 = bf16[16,2,512]{2,1,0:T(2,128)(2,1)S(1)} async-done(((bf16[16,2,512]{2,1,0:T(2,128)(2,1)}), bf16[16,2,512]{2,1,0:T(2,128)(2,1)S(1)}, u32[]{:S(2)}, u32[]{:S(2)}) %all-to-all-start.8) | async-done | bytes 32800 | tf_op jit(solution)/shard_map/all_to_all | solution.py:75
  522.5 4.0 all-to-all-start.6
  529.2 20.4 %all-to-all-done.6 = f32[16,16,512]{2,1,0:T(8,128)S(1)} async-done(((f32[16,16,512]{2,1,0:T(8,128)}), f32[16,16,512]{2,1,0:T(8,128)S(1)}, u32[]{:S(2)}, u32[]{:S(2)}) %all-to-all-start.6) | async-done | bytes 524320 | tf_op jit(solution)/shard_map/all_to_all | solution.py:75
  549.6 10.0 %all-to-all-start.5 = ((bf16[16,64,512]{2,1,0:T(8,128)(2,1)}), bf16[16,64,512]{2,1,0:T(8,128)(2,1)S(1)}, u32[]{:S(2)}, u32[]{:S(2)}) async-start(bf16[16,64,512]{2,1,0:T(8,128)(2,1)} %bitcast.196), calls=%async_computation.5 | async-start | bytes 2097152 | tf_op jit(solution)/shard_map/all_to_all | solution.py:37
  567.4 20.3 %all-to-all-done.5 = bf16[16,64,512]{2,1,0:T(8,128)(2,1)S(1)} async-done(((bf16[16,64,512]{2,1,0:T(8,128)(2,1)}), bf16[16,64,512]{2,1,0:T(8,128)(2,1)S(1)}, u32[]{:S(2)}, u32[]{:S(2)}) %all-to-all-start.5) | async-done | bytes 1048608 | tf_op jit(solution)/shard_map/all_to_all | solution.py:37
  587.9 3.7 copy.135
  (156 shorter events, 58.6 us)
Async XLA Ops:
  7.2 129.8 %copy-start = (bf16[512,512]{1,0:T(8,128)(2,1)S(1)}, bf16[512,512]{1,0:T(8,128)(2,1)}, u32[]{:S(2)}) copy-start(bf16[512,512]{1,0:T(8,128)(2,1)} %param.12) | copy-start | bytes 1572868
  7.2 83.3 %all-gather.8.cloned.1.call-start = ((), (), s32[]{:S(2)}) async-start(), calls=%async_computation.9 | async-start | bytes 2228224 | tf_op jit(solution)/shard_map/all_gather | solution.py:18
  8.9 99.0 %copy-start.18 = (bf16[512,512]{1,0:T(8,128)(2,1)S(1)}, bf16[512,512]{1,0:T(8,128)(2,1)}, u32[]{:S(2)}) copy-start(bf16[512,512]{1,0:T(8,128)(2,1)} %param.14) | copy-start | bytes 1572868
  94.8 26.9 %all-to-all-start = ((bf16[16,64,128]{2,1,0:T(8,128)(2,1)}), bf16[16,64,128]{2,1,0:T(8,128)(2,1)S(1)}, u32[]{:S(2)}, u32[]{:S(2)}) async-start(bf16[16,64,128]{2,1,0:T(8,128)(2,1)} %bitcast.4), calls=%async_computation | async-start | bytes 524288 | tf_op jit(solution)/shard_map/all_to_all | solution.py:37
  121.7 58.8 %all-to-all-start.2 = ((bf16[16,64,512]{2,1,0:T(8,128)(2,1)}), bf16[16,64,512]{2,1,0:T(8,128)(2,1)S(1)}, u32[]{:S(2)}, u32[]{:S(2)}) async-start(bf16[16,64,512]{2,1,0:T(8,128)(2,1)} %bitcast.13), calls=%async_computation.2 | async-start | bytes 2097152 | tf_op jit(solution)/shard_map/all_to_all | solution.py:37
  132.1 90.4 %all-gather.12.cloned.1.call-start = ((), (), s32[]{:S(2)}) async-start(), calls=%async_computation.11 | async-start | bytes 1114112 | tf_op jit(solution)/shard_map/all_gather | solution.py:26
  134.5 168.2 %all-gather.10.cloned.1.call-start = ((), (), s32[]{:S(2)}) async-start(), calls=%async_computation.10 | async-start | bytes 3342336 | tf_op jit(solution)/shard_map/all_gather | solution.py:26
  180.6 63.1 %all-to-all-start.1 = ((bf16[16,64,512]{2,1,0:T(8,128)(2,1)}), bf16[16,64,512]{2,1,0:T(8,128)(2,1)S(1)}, u32[]{:S(2)}, u32[]{:S(2)}) async-start(bf16[16,64,512]{2,1,0:T(8,128)(2,1)} %bitcast.204), calls=%async_computation.1 | async-start | bytes 2097152 | tf_op jit(solution)/shard_map/all_to_all | solution.py:37
  194.6 113.6 %copy-start.12 = (f32[64]{0:T(128)}, f32[64]{0:T(128)S(1)}, u32[]{:S(2)}) copy-start(f32[64]{0:T(128)S(1)} %multiply_exponential_fusion.1) | copy-start | bytes 772
  194.6 113.6 %copy-start.14 = (pred[64]{0:T(512)(128)(4,1)}, pred[64]{0:T(512)(128)(4,1)S(1)}, u32[]{:S(2)}) copy-start(pred[64]{0:T(512)(128)(4,1)S(1)} %broadcast_compare_fusion.1) | copy-start | bytes 196
  194.6 157.4 %copy-start.16 = (pred[512]{0:T(512)(128)(4,1)}, pred[512]{0:T(512)(128)(4,1)S(1)}, u32[]{:S(2)}) copy-start(pred[512]{0:T(512)(128)(4,1)S(1)} %broadcast_compare_fusion) | copy-start | bytes 1540
  307.1 46.5 %copy-start.6 = (pred[64,1024]{1,0:T(8,128)(4,1)S(1)}, pred[64,1024]{1,0:T(8,128)(4,1)}, u32[]{:S(2)}) copy-start(pred[64,1024]{1,0:T(8,128)(4,1)} %iota_compare_fusion) | copy-start | bytes 196612
  330.7 26.8 %collective-permute-start.1 = (bf16[1024,64]{1,0:T(8,128)(2,1)S(1)}, bf16[1024,64]{1,0:T(8,128)(2,1)S(1)}, u32[]{:S(2)}, u32[]{:S(2)}) collective-permute-start(bf16[1024,64]{1,0:T(8,128)(2,1)S(1)} %get-tuple-element.6), channel_id=1, source_target_pairs={{0,16},{16,0},{32,48},{48,32},{64,80},{80,64},{96,112},{112,96},{1... | collective-permute-start | bytes 393224 | tf_op jit(solution)/shard_map/ppermute | solution.py:49
  350.1 3.5 collective-permute-start
  355.1 6.6 %collective-permute-start.3 = (f32[1024,64]{0,1:T(8,128)S(1)}, f32[1024,64]{0,1:T(8,128)S(1)}, u32[]{:S(2)}, u32[]{:S(2)}) collective-permute-start(f32[1024,64]{0,1:T(8,128)S(1)} %dynamic-slice_bitcast_fusion), channel_id=1, source_target_pairs={{0,16},{16,0},{32,48},{48,32},{64,80},{80,64},{96,112},{112,96},{1... | collective-permute-start | bytes 786440 | tf_op jit(solution)/shard_map/ppermute | solution.py:49
  359.4 3.6 collective-permute-start.2
  365.1 29.4 %all-to-all-start.4 = ((f32[16,64,128]{2,1,0:T(8,128)}), f32[16,64,128]{2,1,0:T(8,128)S(1)}, u32[]{:S(2)}, u32[]{:S(2)}) async-start(f32[16,64,128]{2,1,0:T(8,128)} %bitcast.41), calls=%async_computation.4 | async-start | bytes 1048576 | tf_op jit(solution)/shard_map/all_to_all | solution.py:54
  395.5 79.4 %all-to-all-start.3 = ((bf16[16,64,512]{2,1,0:T(8,128)(2,1)}), bf16[16,64,512]{2,1,0:T(8,128)(2,1)S(1)}, u32[]{:S(2)}, u32[]{:S(2)}) async-start(bf16[16,64,512]{2,1,0:T(8,128)(2,1)} %broadcast_in_dim.46), calls=%async_computation.3 | async-start | bytes 2097152 | tf_op jit(solution)/shard_map/all_to_all | solution.py:75
  408.6 67.5 %copy-start.5 = (bf16[128,4,64]{0,2,1:T(8,128)(2,1)S(1)}, bf16[128,4,64]{0,2,1:T(8,128)(2,1)}, u32[]{:S(2)}) copy-start(bf16[128,4,64]{0,2,1:T(8,128)(2,1)} %get-tuple-element.27) | copy-start | bytes 196612
  408.6 179.3 %all-gather.14.cloned.1.call-start = ((), (), s32[]{:S(2)}) async-start(), calls=%async_computation.12 | async-start | bytes 3342336 | tf_op jit(solution)/shard_map/all_gather | solution.py:26
  475.3 51.2 %copy-start.3 = (bf16[2,512,64]{1,2,0:T(8,128)(2,1)S(1)}, bf16[2,512,64]{1,2,0:T(8,128)(2,1)}, u32[]{:S(2)}) copy-start(bf16[2,512,64]{1,2,0:T(8,128)(2,1)} %param.13) | copy-start | bytes 393220
  500.0 21.7 %all-to-all-start.8 = ((bf16[16,2,512]{2,1,0:T(2,128)(2,1)}), bf16[16,2,512]{2,1,0:T(2,128)(2,1)S(1)}, u32[]{:S(2)}, u32[]{:S(2)}) async-start(bf16[16,2,512]{2,1,0:T(2,128)(2,1)} %reshape.373), calls=%async_computation.8 | async-start | bytes 65536 | tf_op jit(solution)/shard_map/all_to_all | solution.py:75
  522.5 27.1 %all-to-all-start.6 = ((f32[16,16,512]{2,1,0:T(8,128)}), f32[16,16,512]{2,1,0:T(8,128)S(1)}, u32[]{:S(2)}, u32[]{:S(2)}) async-start(f32[16,16,512]{2,1,0:T(8,128)} %broadcast_in_dim.47), calls=%async_computation.6 | async-start | bytes 1048576 | tf_op jit(solution)/shard_map/all_to_all | solution.py:75
  549.6 38.1 %all-to-all-start.5 = ((bf16[16,64,512]{2,1,0:T(8,128)(2,1)}), bf16[16,64,512]{2,1,0:T(8,128)(2,1)S(1)}, u32[]{:S(2)}, u32[]{:S(2)}) async-start(bf16[16,64,512]{2,1,0:T(8,128)(2,1)} %bitcast.196), calls=%async_computation.5 | async-start | bytes 2097152 | tf_op jit(solution)/shard_map/all_to_all | solution.py:37
  (14 other events, 163.9 us)
Sparse Core Ops, SparseCore 0:
  10.2 80.2 all-gather.7
  135.6 86.8 all-gather.11
  224.7 77.9 all-gather.9
  476.2 52.4 all-gather.13
where the time goes:
time: 602 us; the launch traced here: 601 us
  waiting for transfers between devices  313 us (52%)
  blocking collectives  109 us (18%)
  starting transfers between devices  108 us (18%)
  matrix products  26.7 us (4%)
  local copies, waits for them, and re-layouts  19.8 us (3%)
  between operations  14.5 us (2%)
  other arithmetic  10.4 us (2%)
    all_to_all x4, waiting for transfers between devices, sum_at_owner(): lax.all_to_all(pieces, axis, split_axis=0, concat_axis=0, tiled=True)  91.2 us
    all_gather x2, blocking collectives, in_one_piece(): lax.all_gather(both, axis, axis=dim, tiled=True)  87.3 us
    all_gather x3, waiting for transfers between devices, gathered_total(): return lax.all_gather(array, axis).sum(0)  85.9 us
    all_gather x1, waiting for transfers between devices, in_one_piece(): lax.all_gather(both, axis, axis=dim, tiled=True)  81.6 us
    all_to_all x4, starting transfers between devices, sum_at_owner(): lax.all_to_all(pieces, axis, split_axis=0, concat_axis=0, tiled=True)  47.3 us
    all_to_all x3, waiting for transfers between devices, from_everyone(): lax.all_to_all(jnp.broadcast_to(array[None], (size, *array.shape)), axis,...  30.9 us
    all_to_all x3, starting transfers between devices, from_everyone(): lax.all_to_all(jnp.broadcast_to(array[None], (size, *array.shape)), axis,...  27.4 us
    ppermute x4, starting transfers between devices, from_partner(): lax.ppermute(array, axis, [(i, i ^ 1 << bit) for i in range(lax.axis_size...  26 us
  transfers between devices with their start and end apart: 16, of which 12 were waited for; matrix products, arithmetic and copies ran while one was open for 6% of the time, Pallas kernels for 0%

commit v1 on v0

v1 whole, which is shorter than its diff:
```python
import math

import jax
import jax.numpy as jnp
from jax import lax
from jax.sharding import PartitionSpec as P

HEAD_DIM = 128
ADAPTER_RANK = 16

adapter_scale = 2.0
rope_base = 500000.0

f32 = jnp.float32
bf16 = jnp.bfloat16


def dot(a, b):
    return jnp.dot(a, b, preferred_element_type=f32)


def dot_nt(a, b):
    return lax.dot_general(a, b, (((1,), (1,)), ((), ())), preferred_element_type=f32)


def dot_tn(a, b):
    return lax.dot_general(a, b, (((0,), (0,)), ((), ())), preferred_element_type=f32)


def by_core(size):
    return [[2 * k + c for k in range(size // 2)] for c in range(2)]


def from_partner(array):
    return lax.ppermute(array, "ffn", [(i, i ^ 1) for i in range(lax.axis_size("ffn"))])


def sent_to_all(array, axis, groups=None):
    size = len(groups[0]) if groups else lax.axis_size(axis)
    copies = jnp.broadcast_to(array[None], (size, *array.shape))
    return lax.all_to_all(copies, axis, 0, 0, tiled=True, axis_index_groups=groups)


def pieces_summed(array, axis, groups=None):
    size = len(groups[0]) if groups else lax.axis_size(axis)
    pieces = array.reshape(size, array.shape[0] // size, *array.shape[1:])
    arrived = lax.all_to_all(pieces, axis, 0, 0, tiled=True, axis_index_groups=groups)
    return arrived.astype(f32).sum(axis=0)


def rope_tables(positions, first_dim, columns):
    dims = (first_dim + jnp.arange(columns, dtype=jnp.int32)) % HEAD_DIM
    pair_dims = dims - dims % 2
    frequency = jnp.exp(pair_dims.astype(f32) * (-math.log(rope_base) / HEAD_DIM))
    angles = positions.astype(f32)[:, None] * frequency[None, :]
    return jnp.cos(angles), jnp.sin(angles)


def rotate(values, tables, direction):
    cos, sin = tables
    is_even = jnp.arange(values.shape[-1], dtype=jnp.int32) % 2 == 0
    following = jnp.roll(values, -1, axis=-1)
    preceding = jnp.roll(values, 1, axis=-1)
    partner = jnp.where(is_even, -following, preceding)
    return values * cos + direction * partner * sin


def shards(
    hidden,
    upstream,
    query_frozen_weight,
    key_value_frozen_weight,
    output_frozen_weight,
    adapter_down,
    query_up_map,
    key_value_up_maps,
    output_down_map,
    output_up,
):
    ffn_count = lax.axis_size("ffn")
    width_count = lax.axis_size("width")
    ffn_index = lax.axis_index("ffn")
    width_index = lax.axis_index("width")
    parity = ffn_index % 2
    same_core = by_core(ffn_count)
    own_rows, width_cols = hidden.shape
    token_count = own_rows * ffn_count
    query_rows = token_count // width_count
    query_cols = query_frozen_weight.shape[1]
    key_cols = key_value_frozen_weight.shape[2]
    heads = query_cols // HEAD_DIM
    rank = ADAPTER_RANK
    score_scale = 1.0 / math.sqrt(HEAD_DIM)
    row_positions = width_index * query_rows + jnp.arange(query_rows, dtype=jnp.int32)

    query_weight = (
        query_frozen_weight.astype(f32) + adapter_scale * dot_tn(adapter_down[0], query_up_map)
    ).astype(bf16)
    key_value_weight = jnp.concatenate(
        [
            key_value_frozen_weight[k].astype(f32)
            + adapter_scale * dot_tn(adapter_down[k + 1], key_value_up_maps[k])
            for k in range(2)
        ],
        axis=1,
    ).astype(bf16)
    output_weight = (
        output_frozen_weight.astype(f32) + adapter_scale * dot_tn(output_down_map, output_up)
    ).astype(bf16)
    down = adapter_down.reshape(3 * rank, width_cols)
    from_hidden = jnp.concatenate(
        [query_weight, jnp.zeros((width_cols, query_cols), bf16), down.T], axis=1
    )
    from_upstream = jnp.concatenate(
        [jnp.zeros((width_cols, query_cols), bf16), output_weight.T], axis=1
    )
    pad = 128
    from_hidden = jnp.pad(from_hidden, ((0, 0), (0, pad - 3 * rank)))
    from_upstream = jnp.concatenate(
        [
            from_upstream,
            jnp.zeros((width_cols, 3 * rank), bf16),
            output_up.T,
            jnp.zeros((width_cols, pad - 4 * rank), bf16),
        ],
        axis=1,
    )
    joint_weight = jnp.concatenate([from_hidden, from_upstream], axis=0)
    query_tables = rope_tables(row_positions, 0, HEAD_DIM)
    key_tables = rope_tables(row_positions, ffn_index * key_cols, key_cols)
    joint_weight, key_value_weight, query_weight, query_tables, key_tables = (
        lax.optimization_barrier(
            (joint_weight, key_value_weight, query_weight, query_tables, key_tables)
        )
    )

    both = jnp.concatenate([hidden, upstream], axis=1)
    own_core = sent_to_all(both, "ffn", same_core)
    other_core = from_partner(own_core)
    rows = jnp.where(
        parity == 0,
        jnp.stack([own_core, other_core], axis=1),
        jnp.stack([other_core, own_core], axis=1),
    ).reshape(token_count, 2 * width_cols)
    hidden_rows = rows[:, :width_cols]
    upstream_rows = rows[:, width_cols:]

    joint_part = dot(rows, joint_weight).astype(bf16)
    joint_rows = lax.psum_scatter(joint_part, "width", scatter_dimension=0, tiled=True)

    key_value_part = dot(hidden_rows, key_value_weight).astype(bf16)
    key_value_sum = pieces_summed(key_value_part, "width")
    key_value_rows = jnp.concatenate(
        [rotate(key_value_sum[:, :key_cols], key_tables, 1.0), key_value_sum[:, key_cols:]], axis=1
    ).astype(bf16)
    own_half = sent_to_all(key_value_rows, "width").reshape(token_count, 2 * key_cols)
    other_half = from_partner(own_half)
    first = jnp.where(parity == 0, own_half, other_half)
    second = jnp.where(parity == 0, other_half, own_half)
    key_states = jnp.concatenate([first[:, :key_cols], second[:, :key_cols]], axis=1)
    value_states = jnp.concatenate([first[:, key_cols:], second[:, key_cols:]], axis=1)

    def by_head(values):
        return values.reshape(query_rows, heads, HEAD_DIM).transpose(1, 0, 2)

    def by_row(values):
        return (
            values.reshape(heads, query_rows, HEAD_DIM)
            .transpose(1, 0, 2)
            .reshape(query_rows, query_cols)
        )

    low_rows = joint_rows[:, 2 * query_cols : 2 * query_cols + 4 * rank]
    query = (
        rotate(by_head(joint_rows[:, :query_cols].astype(f32)), query_tables, 1.0)
        .astype(bf16)
        .reshape(heads * query_rows, HEAD_DIM)
    )
    grad = by_head(joint_rows[:, query_cols : 2 * query_cols]).reshape(
        heads * query_rows, HEAD_DIM
    )
    positions = jnp.arange(token_count, dtype=jnp.int32)
    causal = jnp.tile(row_positions, heads)[:, None] >= positions[None, :]
    scores = jnp.where(causal, dot_nt(query, key_states) * score_scale, -jnp.inf)
    shifted = jnp.exp(scores - jnp.max(scores, axis=-1, keepdims=True))
    probs = shifted / jnp.sum(shifted, axis=-1, keepdims=True)
    prob_weights = probs.astype(bf16)
    attention = dot(prob_weights, value_states).astype(bf16)
    prob_grad = dot_nt(grad, value_states)
    delta = jnp.sum(grad.astype(f32) * attention.astype(f32), axis=-1, keepdims=True)
    score_grad = (probs * (prob_grad - delta) * score_scale).astype(bf16)
    query_grad = by_row(
        rotate(
            dot(score_grad, key_states).reshape(heads, query_rows, HEAD_DIM), query_tables, -1.0
        ).astype(bf16)
    )
    key_part_grad = dot_tn(score_grad, query)
    value_part_grad = dot_tn(prob_weights, grad)
    attention_rows = by_row(attention)

    output_down_part = dot_tn(low_rows[:, 3 * rank :], attention_rows).astype(bf16)
    riding = jnp.concatenate(
        [query_grad, output_down_part.reshape(query_rows, -1), low_rows], axis=1
    )
    gathered = lax.all_gather(riding, "width", axis=0, tiled=True)

    def halves(own):
        start = jnp.where(own, parity, 1 - parity) * key_cols
        return jnp.concatenate(
            [
                lax.dynamic_slice_in_dim(key_part_grad, start, key_cols, 1),
                lax.dynamic_slice_in_dim(value_part_grad, start, key_cols, 1),
            ],
            axis=1,
        )

    received = from_partner(halves(False).astype(bf16))
    key_value_total = (halves(True) + received.astype(f32)).astype(bf16)
    key_value_grad_sum = pieces_summed(key_value_total, "width")
    key_grad = rotate(key_value_grad_sum[:, :key_cols], key_tables, -1.0).astype(bf16)
    value_grad = key_value_grad_sum[:, key_cols:].astype(bf16)
    terms = jnp.concatenate(
        [
            dot_nt(query_grad, query_up_map),
            dot_nt(key_grad, key_value_up_maps[0]),
            dot_nt(value_grad, key_value_up_maps[1]),
            dot_nt(attention_rows, output_down_map),
        ],
        axis=1,
    )
    terms = terms + from_partner(terms)
    terms = sent_to_all(terms, "ffn", same_core).sum(axis=0).astype(bf16)
    key_value_riding = jnp.concatenate([key_grad, value_grad, terms], axis=1)
    key_value_gathered = sent_to_all(key_value_riding, "width").reshape(token_count, -1)

    query_grad_rows = gathered[:, :query_cols]
    key_value_grad_rows = key_value_gathered[:, : 2 * key_cols]

    input_part = dot_nt(query_grad_rows, query_weight) + dot_nt(
        key_value_grad_rows, key_value_weight
    )
    by_owner = input_part.reshape(ffn_count // 2, 2, own_rows, width_cols)
    kept = lax.dynamic_index_in_dim(by_owner, parity, 1, keepdims=False)
    given = lax.dynamic_index_in_dim(by_owner, 1 - parity, 1, keepdims=False).astype(bf16)
    pair_sum = (kept + from_partner(given).astype(f32)).astype(bf16)
    hidden_gradient = pieces_summed(
        pair_sum.reshape(ffn_count // 2 * own_rows, width_cols), "ffn", same_core
    ).astype(bf16)

    low = gathered[:, query_cols + 2 * key_cols :]
    rank_gradient = key_value_gathered[:, 2 * key_cols : 2 * key_cols + 3 * rank]
    outer_rank = key_value_gathered[:, 2 * key_cols + 3 * rank :]
    down_map_gradient = (adapter_scale * dot_tn(rank_gradient, hidden_rows)).reshape(
        adapter_down.shape
    )
    query_up_map_gradient = adapter_scale * dot_tn(low[:, :rank], query_grad_rows)
    key_value_up_maps_gradient = adapter_scale * jnp.stack(
        [
            dot_tn(low[:, rank : 2 * rank], key_value_grad_rows[:, :key_cols]),
            dot_tn(low[:, 2 * rank : 3 * rank], key_value_grad_rows[:, key_cols:]),
        ]
    )
    output_down_map_gradient = adapter_scale * gathered[
        :, query_cols : query_cols + 2 * key_cols
    ].reshape(width_count, query_rows, 2 * key_cols).astype(f32).sum(axis=0).reshape(
        rank, query_cols
    )
    output_up_map_gradient = adapter_scale * dot_tn(outer_rank, upstream_rows)
    return (
        hidden_gradient,
        down_map_gradient,
        query_up_map_gradient,
        key_value_up_maps_gradient,
        output_down_map_gradient,
        output_up_map_gradient,
    )


def solution(mesh):
    placed = (
        P(("groups", "ffn"), "width"),
        P(("groups", "ffn"), "width"),
        P("width", "ffn"),
        P(None, "width", "ffn"),
        P("ffn", "width"),
        P("groups", None, "width"),
        P("groups", "ffn"),
        P("groups", None, "ffn"),
        P("groups", "ffn"),
        P("groups", "width"),
    )
    return jax.shard_map(
        shards,
        mesh=mesh,
        in_specs=placed,
        out_specs=(
            P(("groups", "ffn"), "width"),
            P("groups", None, "width"),
            P("groups", "ffn"),
            P("groups", None, "ffn"),
            P("groups", "ffn"),
            P("groups", "width"),
        ),
        check_vma=False,
    )
```

time: 602 us -> 336 us (0.56)
  waiting for transfers between devices: 313 us -> 113 us
  blocking collectives: 109 us -> 28.5 us
  starting transfers between devices: 108 us -> 127 us
  local copies, waits for them, and re-layouts: 19.8 us -> 13.5 us
    all_gather x4 -> x1, waiting for transfers between devices: 168 us -> 7.88 us  [shards(): gathered = lax.all_gather(riding, 'width', axis=0, tiled=True)]
    all_gather x2 -> x0, blocking collectives: 87.3 us -> none  [in_one_piece(): lax.all_gather(both, axis, axis=dim, tiled=True)]
    all_to_all x8 -> x6, waiting for transfers between devices: 143 us -> 89.3 us  [the longest x3 50.6 us: sent_to_all(): lax.all_to_all(copies, axis, 0, 0, tiled=True, axis_index_groups=groups)]
    ppermute x4 -> x5, starting transfers between devices: 26 us -> 74.8 us  [from_partner(): lax.ppermute(array, 'ffn', [(i, i ^ 1) for i in range(lax.axis_size('ffn'...]
    all_to_all x8 -> x6, starting transfers between devices: 81.5 us -> 52.1 us  [the longest x3 33.6 us: pieces_summed(): lax.all_to_all(pieces, axis, 0, 0, tiled=True, axis_index_groups=groups)]
    reduce_scatter x0 -> x1, waiting for transfers between devices: none -> 14.1 us  [shards(): lax.psum_scatter(joint_part, 'width', scatter_dimension=0, tiled=True)]
    all_to_all x1, blocking collectives: 21.4 us -> 28.5 us  [sent_to_all(): lax.all_to_all(copies, axis, 0, 0, tiled=True, axis_index_groups=groups)]
    unnamed x54 -> x78, local copies, waits for them, and re-layouts: 12 us -> 5 us
  transfers between devices with their start and end apart: 16 -> 13, of which waited for: 12 -> 10; matrix products, arithmetic and copies ran while one was open for 6% -> 7% of each run, Pallas kernels for 0% -> 0%
where the time goes in v1:
time: 336 us; the launch traced here: 335 us
  starting transfers between devices  127 us (38%)
  waiting for transfers between devices  113 us (34%)
  blocking collectives  28.5 us (8%)
  matrix products  23.6 us (7%)
  between operations  15 us (4%)
  other arithmetic  13.9 us (4%)
  local copies, waits for them, and re-layouts  13.5 us (4%)
    ppermute x5, starting transfers between devices, from_partner(): lax.ppermute(array, 'ffn', [(i, i ^ 1) for i in range(lax.axis_size('ffn'...  74.8 us
    all_to_all x3, waiting for transfers between devices, sent_to_all(): lax.all_to_all(copies, axis, 0, 0, tiled=True, axis_index_groups=groups)  50.6 us
    all_to_all x3, waiting for transfers between devices, pieces_summed(): lax.all_to_all(pieces, axis, 0, 0, tiled=True, axis_index_groups=groups)  38.7 us
    all_to_all x3, starting transfers between devices, pieces_summed(): lax.all_to_all(pieces, axis, 0, 0, tiled=True, axis_index_groups=groups)  33.6 us
    all_to_all x1, blocking collectives, sent_to_all(): lax.all_to_all(copies, axis, 0, 0, tiled=True, axis_index_groups=groups)  28.5 us
    all_to_all x3, starting transfers between devices, sent_to_all(): lax.all_to_all(copies, axis, 0, 0, tiled=True, axis_index_groups=groups)  18.5 us
    reduce_scatter x1, waiting for transfers between devices, shards(): lax.psum_scatter(joint_part, 'width', scatter_dimension=0, tiled=True)  14.1 us
    dot_general x12, matrix products, dot_tn(): lax.dot_general(a, b, (((0,), (0,)), ((), ())), preferred_element_type=f32)  8.75 us
  transfers between devices with their start and end apart: 13, of which 10 were waited for; matrix products, arithmetic and copies ran while one was open for 7% of the time, Pallas kernels for 0%

profile of v1, /device:TPU:65, one launch (start us, length us, event | category | flops | bytes accessed | tf_op | source)
XLA Modules:
  0.0 334.6 jit_solution(8557260384772392533)
XLA Ops:
  9.3 8.0 %all-to-all-start = ((bf16[8,64,1024]{2,1,0:T(8,128)(2,1)}), bf16[8,64,1024]{2,1,0:T(8,128)(2,1)S(1)}, u32[]{:S(2)}, u32[]{:S(2)}) async-start(bf16[8,64,1024]{2,1,0:T(8,128)(2,1)} %broadcast_in_dim.30), calls=%async_computation | async-start | bytes 2097152 | tf_op jit(solution)/shard_map/all_to_all | solution.py:41
  19.3 15.8 %all-to-all-done = bf16[8,64,1024]{2,1,0:T(8,128)(2,1)S(1)} async-done(((bf16[8,64,1024]{2,1,0:T(8,128)(2,1)}), bf16[8,64,1024]{2,1,0:T(8,128)(2,1)S(1)}, u32[]{:S(2)}, u32[]{:S(2)}) %all-to-all-start) | async-done | bytes 1048608 | tf_op jit(solution)/shard_map/all_to_all | solution.py:41
  35.1 40.2 %collective-permute-start = (bf16[8,64,1024]{2,1,0:T(8,128)(2,1)S(1)}, bf16[8,64,1024]{2,1,0:T(8,128)(2,1)}, u32[]{:S(2)}, u32[]{:S(2)}) collective-permute-start(bf16[8,64,1024]{2,1,0:T(8,128)(2,1)S(1)} %all-to-all-done), channel_id=1, source_target_pairs={{0,16},{16,0},{32,48},{48,32},{64,80},{80,64},{96,112},{112,96},{1... | collective-permute-start | bytes 3145736 | tf_op jit(solution)/shard_map/ppermute | solution.py:35
  78.7 1.8 maximum_select_fusion
  80.6 4.2 %convolution_convert_fusion = bf16[1024,1152]{1,0:T(8,128)(2,1)} fusion(bf16[1024,1024]{1,0:T(8,128)(2,1)S(1)} %bitcast.108, bf16[1024,1152]{0,1:T(8,128)(2,1)S(1)} %pad_maximum_fusion), kind=kOutput, calls=%fused_computation | convolution fusion | flops 2417098752 | bytes 6815744 | tf_op jit(solution)/shard_map/dot_general | solution.py:19
  86.0 17.0 %all-to-all-start.1 = ((bf16[16,64,128]{2,1,0:T(8,128)(2,1)}), bf16[16,64,128]{2,1,0:T(8,128)(2,1)S(1)}, u32[]{:S(2)}, u32[]{:S(2)}) async-start(bf16[16,64,128]{2,1,0:T(8,128)(2,1)} %bitcast.16), calls=%async_computation.2 | async-start | bytes 524288 | tf_op jit(solution)/shard_map/all_to_all | solution.py:47
  103.0 14.1 %all-to-all-done.1 = bf16[16,64,128]{2,1,0:T(8,128)(2,1)S(1)} async-done(((bf16[16,64,128]{2,1,0:T(8,128)(2,1)}), bf16[16,64,128]{2,1,0:T(8,128)(2,1)S(1)}, u32[]{:S(2)}, u32[]{:S(2)}) %all-to-all-start.1) | async-done | bytes 262176 | tf_op jit(solution)/shard_map/all_to_all | solution.py:47
  117.7 28.5 %all_to_all.35 = bf16[16,64,128]{2,1,0:T(8,128)(2,1)S(1)} all-to-all(bf16[16,64,128]{2,1,0:T(8,128)(2,1)S(1)} %broadcast_in_dim.35), channel_id=1, replica_groups=mesh['groups'=2,'ffn'=16,'width'=16] {'width'}, dimensions={0} | all-to-all | bytes 524288 | tf_op jit(solution)/shard_map/all_to_all | solution.py:41
  146.2 6.9 %collective-permute-start.1 = (bf16[1024,128]{1,0:T(8,128)(2,1)S(1)}, bf16[1024,128]{1,0:T(8,128)(2,1)S(1)}, u32[]{:S(2)}, u32[]{:S(2)}) collective-permute-start(bf16[1024,128]{1,0:T(8,128)(2,1)S(1)} %bitcast.129), channel_id=1, source_target_pairs={{0,16},{16,0},{32,48},{48,32},{64,80},{80,64},{96,112},{112,96},{1... | collective-permute-start | bytes 786440 | tf_op jit(solution)/shard_map/ppermute | solution.py:35
  156.0 14.1 %reduce-scatter.2.cloned.1.call-done = bf16[64,1152]{1,0:T(8,128)(2,1)} async-done(((bf16[1024,1152]{1,0:T(8,128)(2,1)}), bf16[64,1152]{1,0:T(8,128)(2,1)}) %reduce-scatter.2.cloned.1.call-update) | async-done | bytes 147472 | tf_op jit(solution)/shard_map/reduce_scatter | solution.py:149
  179.4 9.4 %collective-permute-start.2 = (bf16[1024,128]{0,1:T(8,128)(2,1)S(1)}, bf16[1024,128]{0,1:T(8,128)(2,1)}, u32[]{:S(2)}, u32[]{:S(2)}) collective-permute-start(bf16[1024,128]{0,1:T(8,128)(2,1)S(1)} %pad_maximum_fusion.3), channel_id=1, source_target_pairs={{0,16},{16,0},{32,48},{48,32},{64,80},{80,64},{96,112},{112,96},{1... | collective-permute-start | bytes 786440 | tf_op jit(solution)/shard_map/ppermute | solution.py:35
  191.9 10.3 %all-to-all-start.3 = ((bf16[16,64,128]{2,1,0:T(8,128)(2,1)}), bf16[16,64,128]{2,1,0:T(8,128)(2,1)S(1)}, u32[]{:S(2)}, u32[]{:S(2)}) async-start(bf16[16,64,128]{2,1,0:T(8,128)(2,1)} %bitcast.24), calls=%async_computation.4 | async-start | bytes 524288 | tf_op jit(solution)/shard_map/all_to_all | solution.py:47
  203.7 12.4 %all-to-all-done.3 = bf16[16,64,128]{2,1,0:T(8,128)(2,1)S(1)} async-done(((bf16[16,64,128]{2,1,0:T(8,128)(2,1)}), bf16[16,64,128]{2,1,0:T(8,128)(2,1)S(1)}, u32[]{:S(2)}, u32[]{:S(2)}) %all-to-all-start.3) | async-done | bytes 262176 | tf_op jit(solution)/shard_map/all_to_all | solution.py:47
  216.7 7.1 %collective-permute-start.3 = (f32[64,64]{0,1:T(8,128)S(1)}, f32[64,64]{0,1:T(8,128)S(1)}, u32[]{:S(2)}, u32[]{:S(2)}) collective-permute-start(f32[64,64]{0,1:T(8,128)S(1)} %pad_maximum_fusion.11), channel_id=1, source_target_pairs={{0,16},{16,0},{32,48},{48,32},{64,80},{80,64},{96,112},{112,96},{1... | collective-permute-start | bytes 49160 | tf_op jit(solution)/shard_map/ppermute | solution.py:35
  225.6 4.6 %all-to-all-start.4 = ((f32[8,1,4096]{2,1,0:T(1,128)}), f32[8,1,4096]{2,1,0:T(1,128)S(1)}, u32[]{:S(2)}, u32[]{:S(2)}) async-start(f32[8,1,4096]{2,1,0:T(1,128)} %reshape.184), calls=%async_computation.5 | async-start | bytes 262144 | tf_op jit(solution)/shard_map/all_to_all | solution.py:41
  230.3 7.9 %all-to-all-done.4 = f32[8,1,4096]{2,1,0:T(1,128)S(1)} async-done(((f32[8,1,4096]{2,1,0:T(1,128)}), f32[8,1,4096]{2,1,0:T(1,128)S(1)}, u32[]{:S(2)}, u32[]{:S(2)}) %all-to-all-start.4) | async-done | bytes 131104 | tf_op jit(solution)/shard_map/all_to_all | solution.py:41
  240.7 5.9 %all-to-all-start.5 = ((bf16[16,64,192]{2,1,0:T(8,128)(2,1)}), bf16[16,64,192]{2,1,0:T(8,128)(2,1)S(1)}, u32[]{:S(2)}, u32[]{:S(2)}) async-start(bf16[16,64,192]{2,1,0:T(8,128)(2,1)} %broadcast_in_dim.68), calls=%async_computation.6 | async-start | bytes 1048576 | tf_op jit(solution)/shard_map/all_to_all | solution.py:41
  246.6 27.0 %all-to-all-done.5 = bf16[16,64,192]{2,1,0:T(8,128)(2,1)S(1)} async-done(((bf16[16,64,192]{2,1,0:T(8,128)(2,1)}), bf16[16,64,192]{2,1,0:T(8,128)(2,1)S(1)}, u32[]{:S(2)}, u32[]{:S(2)}) %all-to-all-start.5) | async-done | bytes 393248 | tf_op jit(solution)/shard_map/all_to_all | solution.py:41
  275.4 7.9 %all-gather.2.cloned.1.call-done = bf16[1024,704]{1,0:T(8,128)(2,1)} async-done(((bf16[64,704]{1,0:T(8,128)(2,1)}), bf16[1024,704]{1,0:T(8,128)(2,1)}) %all-gather.2.cloned.1.call-update) | async-done | bytes 1441808 | tf_op jit(solution)/shard_map/all_gather | solution.py:205
  283.3 2.6 convolution_add_fusion
  288.1 11.2 %collective-permute-start.4 = (bf16[8,64,512]{2,1,0:T(8,128)(2,1)}, bf16[8,64,512]{2,1,0:T(8,128)(2,1)S(1)}, u32[]{:S(2)}, u32[]{:S(2)}) collective-permute-start(bf16[8,64,512]{2,1,0:T(8,128)(2,1)} %fusion.27), channel_id=1, source_target_pairs={{0,16},{16,0},{32,48},{48,32},{64,80},{80,64},{96,112},{112,96},{1... | collective-permute-start | bytes 1572872 | tf_op jit(solution)/shard_map/ppermute | solution.py:35
  299.4 2.3 convolution_multiply_fusion.7
  302.8 6.2 %all-to-all-start.6 = ((bf16[8,64,512]{2,1,0:T(8,128)(2,1)}), bf16[8,64,512]{2,1,0:T(8,128)(2,1)S(1)}, u32[]{:S(2)}, u32[]{:S(2)}) async-start(bf16[8,64,512]{2,1,0:T(8,128)(2,1)} %fusion.20), calls=%async_computation.7 | async-start | bytes 1048576 | tf_op jit(solution)/shard_map/all_to_all | solution.py:47
  314.8 12.2 %all-to-all-done.6 = bf16[8,64,512]{2,1,0:T(8,128)(2,1)S(1)} async-done(((bf16[8,64,512]{2,1,0:T(8,128)(2,1)}), bf16[8,64,512]{2,1,0:T(8,128)(2,1)S(1)}, u32[]{:S(2)}, u32[]{:S(2)}) %all-to-all-start.6) | async-done | bytes 524320 | tf_op jit(solution)/shard_map/all_to_all | solution.py:47
  (182 shorter events, 41.9 us)
Async XLA Ops:
  9.3 25.8 %all-to-all-start = ((bf16[8,64,1024]{2,1,0:T(8,128)(2,1)}), bf16[8,64,1024]{2,1,0:T(8,128)(2,1)S(1)}, u32[]{:S(2)}, u32[]{:S(2)}) async-start(bf16[8,64,1024]{2,1,0:T(8,128)(2,1)} %broadcast_in_dim.30), calls=%async_computation | async-start | bytes 2097152 | tf_op jit(solution)/shard_map/all_to_all | solution.py:41
  17.3 59.7 %copy-start.26 = (bf16[16,512]{1,0:T(8,128)(2,1)S(1)}, bf16[16,512]{1,0:T(8,128)(2,1)}, u32[]{:S(2)}) copy-start(bf16[16,512]{1,0:T(8,128)(2,1)} %param.16) | copy-start | bytes 49156
  17.3 152.8 %reduce-scatter.2.cloned.1.call-start = ((), (), s32[]{:S(2)}) async-start(), calls=%async_computation.8 | async-start | bytes 2506752 | tf_op jit(solution)/shard_map/reduce_scatter | solution.py:149
  18.0 99.4 %copy-start.15 = (f32[64,64]{1,0:T(8,128)}, f32[64,64]{1,0:T(8,128)S(1)}, u32[]{:S(2)}) copy-start(f32[64,64]{1,0:T(8,128)S(1)} %get-tuple-element.18) | copy-start | bytes 49156
  18.0 99.4 %copy-start.17 = (f32[64,64]{1,0:T(8,128)}, f32[64,64]{1,0:T(8,128)S(1)}, u32[]{:S(2)}) copy-start(f32[64,64]{1,0:T(8,128)S(1)} %get-tuple-element.17) | copy-start | bytes 49156
  18.9 135.4 %copy-start.20 = (f32[64,128]{1,0:T(8,128)}, f32[64,128]{1,0:T(8,128)S(1)}, u32[]{:S(2)}) copy-start(f32[64,128]{1,0:T(8,128)S(1)} %get-tuple-element.15) | copy-start | bytes 98308
  35.1 43.7 %collective-permute-start = (bf16[8,64,1024]{2,1,0:T(8,128)(2,1)S(1)}, bf16[8,64,1024]{2,1,0:T(8,128)(2,1)}, u32[]{:S(2)}, u32[]{:S(2)}) collective-permute-start(bf16[8,64,1024]{2,1,0:T(8,128)(2,1)S(1)} %all-to-all-done), channel_id=1, source_target_pairs={{0,16},{16,0},{32,48},{48,32},{64,80},{80,64},{96,112},{112,96},{1... | collective-permute-start | bytes 3145736 | tf_op jit(solution)/shard_map/ppermute | solution.py:35
  86.0 31.2 %all-to-all-start.1 = ((bf16[16,64,128]{2,1,0:T(8,128)(2,1)}), bf16[16,64,128]{2,1,0:T(8,128)(2,1)S(1)}, u32[]{:S(2)}, u32[]{:S(2)}) async-start(bf16[16,64,128]{2,1,0:T(8,128)(2,1)} %bitcast.16), calls=%async_computation.2 | async-start | bytes 524288 | tf_op jit(solution)/shard_map/all_to_all | solution.py:47
  103.0 43.2 %copy-start.32 = (pred[64]{0:T(512)(128)(4,1)}, pred[64]{0:T(512)(128)(4,1)S(1)}, u32[]{:S(2)}) copy-start(pred[64]{0:T(512)(128)(4,1)S(1)} %fusion.85) | copy-start | bytes 196
  146.2 8.7 %collective-permute-start.1 = (bf16[1024,128]{1,0:T(8,128)(2,1)S(1)}, bf16[1024,128]{1,0:T(8,128)(2,1)S(1)}, u32[]{:S(2)}, u32[]{:S(2)}) collective-permute-start(bf16[1024,128]{1,0:T(8,128)(2,1)S(1)} %bitcast.129), channel_id=1, source_target_pairs={{0,16},{16,0},{32,48},{48,32},{64,80},{80,64},{96,112},{112,96},{1... | collective-permute-start | bytes 786440 | tf_op jit(solution)/shard_map/ppermute | solution.py:35
  179.4 10.7 %collective-permute-start.2 = (bf16[1024,128]{0,1:T(8,128)(2,1)S(1)}, bf16[1024,128]{0,1:T(8,128)(2,1)}, u32[]{:S(2)}, u32[]{:S(2)}) collective-permute-start(bf16[1024,128]{0,1:T(8,128)(2,1)S(1)} %pad_maximum_fusion.3), channel_id=1, source_target_pairs={{0,16},{16,0},{32,48},{48,32},{64,80},{80,64},{96,112},{112,96},{1... | collective-permute-start | bytes 786440 | tf_op jit(solution)/shard_map/ppermute | solution.py:35
  191.0 25.2 %copy-start.16 = (f32[64,64]{1,0:T(8,128)S(1)}, f32[64,64]{1,0:T(8,128)}, u32[]{:S(2)}) copy-start(f32[64,64]{1,0:T(8,128)} %copy-done.15) | copy-start | bytes 49156
  191.1 25.2 %copy-start.18 = (f32[64,64]{1,0:T(8,128)S(1)}, f32[64,64]{1,0:T(8,128)}, u32[]{:S(2)}) copy-start(f32[64,64]{1,0:T(8,128)} %copy-done.17) | copy-start | bytes 49156
  191.1 25.2 %copy-start.33 = (pred[64]{0:T(512)(128)(4,1)S(1)}, pred[64]{0:T(512)(128)(4,1)}, u32[]{:S(2)}) copy-start(pred[64]{0:T(512)(128)(4,1)} %copy-done.32) | copy-start | bytes 196
  191.1 25.3 %copy-start.30 = (bf16[2,16,64]{2,1,0:T(8,128)(2,1)S(1)}, bf16[2,16,64]{2,1,0:T(8,128)(2,1)}, u32[]{:S(2)}) copy-start(bf16[2,16,64]{2,1,0:T(8,128)(2,1)} %param.17) | copy-start | bytes 12292
  191.9 24.1 %all-to-all-start.3 = ((bf16[16,64,128]{2,1,0:T(8,128)(2,1)}), bf16[16,64,128]{2,1,0:T(8,128)(2,1)S(1)}, u32[]{:S(2)}, u32[]{:S(2)}) async-start(bf16[16,64,128]{2,1,0:T(8,128)(2,1)} %bitcast.24), calls=%async_computation.4 | async-start | bytes 524288 | tf_op jit(solution)/shard_map/all_to_all | solution.py:47
  202.2 81.0 %all-gather.2.cloned.1.call-start = ((), (), s32[]{:S(2)}) async-start(), calls=%async_computation.9 | async-start | bytes 1671168 | tf_op jit(solution)/shard_map/all_gather | solution.py:205
  216.2 57.4 %copy-start.12 = (bf16[512,128]{0,1:T(8,128)(2,1)S(1)}, bf16[512,128]{0,1:T(8,128)(2,1)}, u32[]{:S(2)}) copy-start(bf16[512,128]{0,1:T(8,128)(2,1)} %copy-done.11) | copy-start | bytes 393220
  216.7 7.9 %collective-permute-start.3 = (f32[64,64]{0,1:T(8,128)S(1)}, f32[64,64]{0,1:T(8,128)S(1)}, u32[]{:S(2)}, u32[]{:S(2)}) collective-permute-start(f32[64,64]{0,1:T(8,128)S(1)} %pad_maximum_fusion.11), channel_id=1, source_target_pairs={{0,16},{16,0},{32,48},{48,32},{64,80},{80,64},{96,112},{112,96},{1... | collective-permute-start | bytes 49160 | tf_op jit(solution)/shard_map/ppermute | solution.py:35
  225.6 12.5 %all-to-all-start.4 = ((f32[8,1,4096]{2,1,0:T(1,128)}), f32[8,1,4096]{2,1,0:T(1,128)S(1)}, u32[]{:S(2)}, u32[]{:S(2)}) async-start(f32[8,1,4096]{2,1,0:T(1,128)} %reshape.184), calls=%async_computation.5 | async-start | bytes 262144 | tf_op jit(solution)/shard_map/all_to_all | solution.py:41
  239.7 43.5 %copy-start.4 = (bf16[512,512]{0,1:T(8,128)(2,1)S(1)}, bf16[512,512]{0,1:T(8,128)(2,1)}, u32[]{:S(2)}) copy-start(bf16[512,512]{0,1:T(8,128)(2,1)} %copy-done.3) | copy-start | bytes 1572868
  240.7 32.9 %all-to-all-start.5 = ((bf16[16,64,192]{2,1,0:T(8,128)(2,1)}), bf16[16,64,192]{2,1,0:T(8,128)(2,1)S(1)}, u32[]{:S(2)}, u32[]{:S(2)}) async-start(bf16[16,64,192]{2,1,0:T(8,128)(2,1)} %broadcast_in_dim.68), calls=%async_computation.6 | async-start | bytes 1048576 | tf_op jit(solution)/shard_map/all_to_all | solution.py:41
  288.1 13.6 %collective-permute-start.4 = (bf16[8,64,512]{2,1,0:T(8,128)(2,1)}, bf16[8,64,512]{2,1,0:T(8,128)(2,1)S(1)}, u32[]{:S(2)}, u32[]{:S(2)}) collective-permute-start(bf16[8,64,512]{2,1,0:T(8,128)(2,1)} %fusion.27), channel_id=1, source_target_pairs={{0,16},{16,0},{32,48},{48,32},{64,80},{80,64},{96,112},{112,96},{1... | collective-permute-start | bytes 1572872 | tf_op jit(solution)/shard_map/ppermute | solution.py:35
  302.8 24.2 %all-to-all-start.6 = ((bf16[8,64,512]{2,1,0:T(8,128)(2,1)}), bf16[8,64,512]{2,1,0:T(8,128)(2,1)S(1)}, u32[]{:S(2)}, u32[]{:S(2)}) async-start(bf16[8,64,512]{2,1,0:T(8,128)(2,1)} %fusion.20), calls=%async_computation.7 | async-start | bytes 1048576 | tf_op jit(solution)/shard_map/all_to_all | solution.py:47
  (27 other events, 278.1 us)
Sparse Core Ops, SparseCore 0:
  84.9 85.1 reduce-scatter.1
  205.8 77.4 all-gather.1
